TPU v7x, 32 devices: a whole 2x2x4 slice. The times are simulated.
32 devices in a mesh: grp: 2 (over y), dev: 16 (over z, x, core).
Axes of the slice: x: 2, y: 2, z: 4, core: 2. Of those that a mesh axis runs over, the one named last changes fastest.
Arguments:
- pooled_grad: bfloat16 [4096, 32, 128], P(('grp', 'dev')), may hold values from -6 to 6
- row_ids: int32 [4096, 4, 32], P(('grp', 'dev')), may hold values from 0 to 1023
- scale_exps: int32 [4096, 32], P(('grp', 'dev')), may hold values from 0 to 3
- table_owner: int32 [32], replicated, may hold values from 0 to 31, each once
- dense_acts: bfloat16 [4096, 512], P(('grp', 'dev')), may hold values from -6 to 6
- dense_cot: bfloat16 [4096, 512], P(('grp', 'dev')), may hold values from -0.1875 to 0.1875
Outputs:
- table_grad: float32 [32, 1024, 128], P('dev')
- weight_grad: float32 [512, 512], replicated
- bias_grad: float32 [512], replicated
Inputs may be any that keep to these rules, and one draw needn't show every extreme that they name: Table t's rows are accumulated into slot table_owner[t]; each slot belongs to exactly one table.
All inputs are finite; a program needn't handle non-finite values.
Results may differ from a plain program's by a relative error of at most 0.0003.
Values may be sent and summed in bfloat16 or wider, within the bound.
A program may use at most 128 MiB of HBM per device.

v0:
```python
import functools

import jax
import jax.numpy as jnp
from jax import lax
from jax.experimental import pallas as pl
from jax.experimental.pallas import tpu as pltpu
from jax.sharding import PartitionSpec as P

ROWS = 1024
DIGIT_BITS = 5
DIGIT = 1 << DIGIT_BITS
MESH = pl.DeviceIdType.MESH
ROW_BLOCK = 256


def powers(exps):
    return (
        1.0
        + (exps >= 1).astype(jnp.float32)
        + 2.0 * (exps >= 2).astype(jnp.float32)
        + 4.0 * (exps >= 3).astype(jnp.float32)
    )


def kernel(
    devs,
    pool,
    slot_ref,
    x_ref,
    ids_ref,
    acts_ref,
    cot_ref,
    table_ref,
    weight_ref,
    bias_ref,
    send,
    recv,
    inter,
    part,
    whole,
    half0,
    half1,
    half2,
    zbuf,
    bpart,
    bhalf,
    bz,
    psend,
    precv,
    csend,
    crecv,
    fsend,
    frecv,
    dsend,
    drecv,
    esend,
    erecv,
    zsend,
    zrecv,
    bsend,
    brecv,
    gsend,
    grecv,
):
    me = lax.axis_index("dev")
    grp = lax.axis_index("grp")
    other = 1 - grp
    owned, samples, feat = table_ref.shape[0], x_ref.shape[1], x_ref.shape[2]
    id_rows = 2 * ids_ref.shape[1]
    zs = devs // 4
    core = lax.rem(me, 2)
    xbit = lax.rem(lax.div(me, 2), 2)
    z = lax.div(me, 4)
    hid, hid2 = weight_ref.shape
    wide = hid2 // 128
    total = hid * wide

    def remote(src, dst, ssem, rsem, dev, group):
        return pltpu.make_async_remote_copy(
            src_ref=src,
            dst_ref=dst,
            send_sem=ssem,
            recv_sem=rsem,
            device_id={"grp": group, "dev": dev},
            device_id_type=MESH,
        )

    def dense_partial():
        for j in range(wide):
            part[pl.ds(j * hid, hid), :] = lax.dot_general(
                acts_ref[...],
                cot_ref[:, j * 128 : (j + 1) * 128],
                (((0,), (0,)), ((), ())),
                preferred_element_type=jnp.float32,
            )
        bpart[0] = jnp.zeros(bpart.shape[1:], jnp.float32)
        for j in range(wide):
            bpart[0, j : j + 1, :] = jnp.sum(
                cot_ref[:, j * 128 : (j + 1) * 128].astype(jnp.float32), axis=0, keepdims=True
            )

    near = me + 1 - 2 * core
    across = me + 2 - 4 * xbit
    stages = (
        (near, grp, core, half0),
        (across, grp, xbit, half1),
        (me, other, grp, half2),
    )
    bases = [0]
    for s in range(3):
        size = total >> (s + 1)
        bases.append(bases[s] + stages[s][2] * size)

    def halving(s):
        dev, group, bit, landing = stages[s]
        size = total >> (s + 1)
        away = pl.multiple_of(bases[s] + (1 - bit) * size, 8)
        return (
            remote(
                part.at[pl.ds(away, size)], landing, dsend.at[s], drecv.at[s], dev, group
            ),
            remote(bpart.at[s], bhalf.at[s], bsend.at[s], brecv.at[s], dev, group),
        )

    def halving_start(s):
        for copy in halving(s):
            copy.start()

    def halving_finish(s):
        for copy in halving(s):
            copy.wait()
        size = total >> (s + 1)
        keep = pl.multiple_of(bases[s + 1], 8)
        part[pl.ds(keep, size), :] = part[pl.ds(keep, size), :] + stages[s][3][...]
        bpart[s + 1] = bpart[s] + bhalf[s]

    piece = (total >> 3) // zs

    def z_copy(k):
        peer = lax.rem(z + k, zs)
        dev = peer * 4 + lax.rem(me, 4)
        away = pl.multiple_of(bases[3] + peer * piece, 8)
        return (
            remote(
                part.at[pl.ds(away, piece)], zbuf.at[z], zsend.at[peer], zrecv.at[z], dev, grp
            ),
            remote(bpart.at[3], bz.at[z], bsend.at[3 + peer], brecv.at[3 + z], dev, grp),
        )

    def z_wait(k):
        peer = lax.rem(z + k, zs)
        dev = peer * 4 + lax.rem(me, 4)
        here = pl.multiple_of(bases[3] + z * piece, 8)
        return (
            remote(
                part.at[pl.ds(here, piece)], zbuf.at[peer], zsend.at[peer], zrecv.at[peer], dev, grp
            ),
            remote(bpart.at[3], bz.at[peer], bsend.at[3 + peer], brecv.at[3 + peer], dev, grp),
        )

    mine = pl.multiple_of(bases[3] + z * piece, 8)

    def z_start():
        @pl.loop(1, zs)
        def _(k):
            for copy in z_copy(k):
                copy.start()

    def z_finish():
        zbuf[z] = part[pl.ds(mine, piece), :]
        bz[z] = bpart[3]

        @pl.loop(1, zs)
        def _(k):
            for copy in z_wait(k):
                copy.wait_recv()

        @pl.loop(1, zs)
        def _(k):
            for copy in z_copy(k):
                copy.wait_send()

        whole[pl.ds(mine, piece), :] = lax.fori_loop(
            1, zs, lambda i, run: run + zbuf[i], zbuf[0]
        )
        bsum = lax.fori_loop(1, zs, lambda i, run: run + bz[i], bz[0])
        for j in range(wide):
            bias_ref[:, j * 128 : (j + 1) * 128] = bsum[j : j + 1, :]

    def zg_copy(k, back):
        peer = lax.rem(z + k, zs)
        dev = peer * 4 + lax.rem(me, 4)
        off = mine if not back else pl.multiple_of(bases[3] + peer * piece, 8)
        block = whole.at[pl.ds(off, piece)]
        return remote(block, block, gsend.at[peer], grecv.at[peer if back else z], dev, grp)

    def zg_start():
        @pl.loop(1, zs)
        def _(k):
            zg_copy(k, False).start()

    def zg_finish():
        @pl.loop(1, zs)
        def _(k):
            zg_copy(k, True).wait_recv()

        @pl.loop(1, zs)
        def _(k):
            zg_copy(k, False).wait_send()

    def doubling(s, back):
        dev, group, bit, _ = stages[s]
        size = total >> (s + 1)
        off = bases[s] + (1 - bit) * size if back else bases[s + 1]
        block = whole.at[pl.ds(pl.multiple_of(off, 8), size)]
        return remote(block, block, esend.at[s], erecv.at[s], dev, group)

    def doubling_start(s):
        doubling(s, False).start()

    def doubling_finish(s):
        doubling(s, True).wait_recv()
        doubling(s, False).wait_send()

    place = lax.rem(me, 4)
    places = (
        place,
        place + 1 - 2 * core,
        place + 2 - 4 * xbit,
        place + 3 - 4 * xbit - 2 * core,
    )

    barrier = pltpu.get_barrier_semaphore()

    def greet(dev, group):
        pl.semaphore_signal(
            barrier, inc=1, device_id={"grp": group, "dev": dev}, device_id_type=MESH
        )

    for m in range(1, 4):
        greet(z * 4 + places[m], grp)

    @pl.loop(1, zs)
    def _(k):
        greet(lax.rem(z + k, zs) * 4 + place, grp)

    greet(me, other)
    pl.semaphore_wait(barrier, 3 + zs)

    def each_far(act):
        @pl.loop(1, zs)
        def _(i):
            for peer in (z + zs - i, z - zs + i):
                pl.when((peer >= 0) & (peer < zs))(functools.partial(act, peer))

    def each_near(act):
        @pl.loop(1, zs)
        def _(i):
            for peer in (z + i, z - i):
                pl.when((peer >= 0) & (peer < zs))(functools.partial(act, peer))

    def column_copy(m, peer):
        return remote(
            send.at[peer * 4 + places[m]],
            inter.at[m - 1, peer],
            psend.at[m - 1, peer],
            precv.at[m - 1, peer],
            z * 4 + places[m],
            grp,
        )

    def level_copy(m, back=False):
        who = z * 4 + places[m]
        return remote(
            send.at[who],
            recv.at[0, who if back else me],
            psend.at[m - 1, z],
            precv.at[m - 1, z],
            who,
            grp,
        )

    def line_copy(m, peer):
        origin = send.at[peer * 4 + place] if m == 0 else inter.at[m - 1, peer]
        return remote(
            origin,
            recv.at[0, z * 4 + places[m]],
            csend.at[m, peer],
            crecv.at[m, z],
            peer * 4 + place,
            grp,
        )

    def line_wait(m, peer):
        landing = recv.at[0, peer * 4 + places[m]]
        remote(
            landing, landing, csend.at[m, peer], crecv.at[m, peer], peer * 4 + place, grp
        ).wait_recv()

    def forward(src):
        return remote(
            recv.at[0, src], recv.at[1, src], fsend.at[src], frecv.at[src], me, other
        )

    def build(dst):
        digits = []
        for s in range(owned):
            t = slot_ref[dst * owned + s]
            send[dst, pl.ds(s * samples, samples), :] = x_ref[t]
            picked = ids_ref[t]
            digits += [picked >> DIGIT_BITS, picked & (DIGIT - 1)]
        send[dst, pl.ds(owned * samples, owned * id_rows), :] = jnp.concatenate(
            digits, axis=0
        ).astype(jnp.float32).astype(jnp.bfloat16)

    pl.loop(0, devs)(build)
    recv[0, me] = send[me]

    def column_start(m):
        each_far(lambda peer: column_copy(m, peer).start())
        level_copy(m).start()

    def column_pass(m):
        def act(peer):
            column_copy(m, peer).wait_recv()
            line_copy(m, peer).start()

        each_far(act)
        level_copy(m, True).wait_recv()
        forward(z * 4 + places[m]).start()

    each_far(lambda peer: line_copy(0, peer).start())
    column_start(2)
    column_start(1)
    forward(me).start()

    def accumulate(side, first, second):
        digits = jnp.concatenate(
            [
                recv[side, c, pl.ds(owned * samples, owned * id_rows), :].astype(jnp.float32)
                for c in (first, second)
            ],
            axis=1,
        )
        for s in range(owned):
            top = digits[s * id_rows : s * id_rows + pool]
            low = digits[s * id_rows + pool : s * id_rows + 2 * pool]
            rows = top * DIGIT + low
            values = jnp.concatenate(
                [recv[side, c, pl.ds(s * samples, samples), :] for c in (first, second)],
                axis=0,
            )
            for block in range(ROWS // ROW_BLOCK):
                local = rows - block * ROW_BLOCK
                local = jnp.where((local >= 0) & (local < ROW_BLOCK), local, -1.0).astype(
                    jnp.bfloat16
                )
                axis = lax.broadcasted_iota(
                    jnp.int32, (ROW_BLOCK, 2 * samples), 0
                ).astype(jnp.float32).astype(jnp.bfloat16)
                one, zero = jnp.bfloat16(1), jnp.bfloat16(0)
                counts = jnp.where(local[0:1] == axis, one, zero)
                for p in range(1, pool):
                    counts = counts + jnp.where(local[p : p + 1] == axis, one, zero)
                span = pl.ds(block * ROW_BLOCK, ROW_BLOCK)
                table_ref[s, span, :] = table_ref[s, span, :] + jnp.dot(
                    counts, values, preferred_element_type=jnp.float32
                )

    def pair(side, half, peer):
        accumulate(side, peer * 4 + places[2 * half], peer * 4 + places[2 * half + 1])

    def line_pass(m):
        def act(peer):
            line_wait(m, peer)
            forward(peer * 4 + places[m]).start()

        each_near(act)

    def own_pairs(half):
        pair(0, half, z)
        each_near(functools.partial(pair, 0, half))

    def far_pair(half, peer):
        for m in (2 * half, 2 * half + 1):
            forward(peer * 4 + places[m]).wait_recv()
        pair(1, half, peer)

    dense_partial()
    halving_start(0)
    column_pass(1)
    table_ref[...] = jnp.zeros(table_ref.shape, jnp.float32)
    halving_finish(0)
    halving_start(1)
    column_start(3)
    column_pass(2)
    line_pass(0)
    halving_finish(1)
    halving_start(2)
    line_pass(1)
    halving_finish(2)
    z_start()
    column_pass(3)
    own_pairs(0)
    line_pass(2)
    z_finish()
    zg_start()
    far_pair(0, z)
    line_pass(3)
    zg_finish()
    doubling_start(2)
    own_pairs(1)
    each_near(functools.partial(far_pair, 0))
    doubling_finish(2)
    doubling_start(1)
    far_pair(1, z)
    each_near(functools.partial(far_pair, 1))
    doubling_finish(1)
    doubling_start(0)
    doubling_finish(0)
    for j in range(wide):
        weight_ref[:, j * 128 : (j + 1) * 128] = whole[pl.ds(j * hid, hid), :]

    def drain(peer):
        for m in range(4):
            line_copy(m, peer).wait_send()
            if m > 0:
                column_copy(m, peer).wait_send()

    each_near(drain)
    for m in range(1, 4):
        level_copy(m).wait_send()

    @pl.loop(0, devs)
    def _(src):
        forward(src).wait_send()


def solution(mesh):
    devs = mesh.shape["dev"]

    def per_device(pooled_grad, row_ids, scale_exps, table_owner, dense_acts, dense_cot):
        samples, tables, feat = pooled_grad.shape
        pool = row_ids.shape[1]
        owned = tables // devs
        hid, hid2 = dense_acts.shape[1], dense_cot.shape[1]
        zs = devs // 4
        factor = powers(scale_exps)[:, :, None]
        restored = jnp.transpose(
            jnp.clip(pooled_grad.astype(jnp.float32), -factor, factor).astype(jnp.bfloat16),
            (1, 0, 2),
        )
        by_table = jnp.transpose(row_ids, (2, 1, 0))
        order = jnp.arange(tables, dtype=jnp.int32)
        slots = jnp.sum(
            jnp.where(table_owner[None, :] == order[:, None], order[None, :], 0), axis=1
        ).astype(jnp.int32)
        rows = owned * samples + owned * 2 * pool
        total = hid * hid2 // 128
        dma = pltpu.SemaphoreType.DMA
        vmem = pl.BlockSpec(memory_space=pltpu.VMEM)
        table_grad, weight_grad, bias_grad = pl.pallas_call(
            functools.partial(kernel, devs, pool),
            out_shape=(
                jax.ShapeDtypeStruct((owned, ROWS, feat), jnp.float32),
                jax.ShapeDtypeStruct((hid, hid2), jnp.float32),
                jax.ShapeDtypeStruct((1, hid2), jnp.float32),
            ),
            in_specs=[pl.BlockSpec(memory_space=pltpu.SMEM)] + [vmem] * 4,
            out_specs=(vmem, vmem, vmem),
            scratch_shapes=[
                pltpu.VMEM((devs, rows, feat), jnp.bfloat16),
                pltpu.VMEM((2, devs, rows, feat), jnp.bfloat16),
                pltpu.VMEM((3, zs, rows, feat), jnp.bfloat16),
                pltpu.VMEM((total, 128), jnp.float32),
                pltpu.VMEM((total, 128), jnp.float32),
                pltpu.VMEM((total // 2, 128), jnp.float32),
                pltpu.VMEM((total // 4, 128), jnp.float32),
                pltpu.VMEM((total // 8, 128), jnp.float32),
                pltpu.VMEM((zs, total // 8 // zs, 128), jnp.float32),
                pltpu.VMEM((4, 8, 128), jnp.float32),
                pltpu.VMEM((3, 8, 128), jnp.float32),
                pltpu.VMEM((zs, 8, 128), jnp.float32),
                dma((3, zs)),
                dma((3, zs)),
                dma((4, zs)),
                dma((4, zs)),
                dma((devs,)),
                dma((devs,)),
                dma((3,)),
                dma((3,)),
                dma((3,)),
                dma((3,)),
                dma((zs,)),
                dma((zs,)),
                dma((3 + zs,)),
                dma((3 + zs,)),
                dma((zs,)),
                dma((zs,)),
            ],
            compiler_params=pltpu.CompilerParams(collective_id=0, has_side_effects=True),
        )(slots, restored, by_table, dense_acts, dense_cot)
        return table_grad, weight_grad, bias_grad.reshape(hid2)

    return jax.shard_map(
        per_device,
        mesh=mesh,
        in_specs=(
            P(("grp", "dev"), None, None),
            P(("grp", "dev"), None, None),
            P(("grp", "dev"), None),
            P(),
            P(("grp", "dev"), None),
            P(("grp", "dev"), None),
        ),
        out_specs=(P("dev", None, None), P(), P()),
        check_vma=False,
    )
```

profile of v0, /device:TPU:0, one launch (start us, length us, event | category | flops | bytes accessed | tf_op | source)
XLA Modules:
  0.0 64.2 jit_solution(4113493788717400083)
XLA Ops:
  0.6 1.3 %select_reduce_fusion.slot_ref = s32[32]{0:T(128)} fusion(s32[32]{0:T(128)} %param.9), kind=kLoop, calls=%fused_computation.4 | loop fusion | flops 3040 | bytes 256 | tf_op jit(solution)/shard_map/reduce_sum | solution.py:456
  1.9 0.7 %select_add_fusion = (bf16[128,32]{0,1:T(8,128)(2,1)S(1)}, bf16[128,32]{0,1:T(8,128)(2,1)S(1)}) fusion(s32[128,32]{0,1:T(8,128)} %param.8), kind=kLoop, calls=%fused_computation.3 | loop fusion | flops 53248 | bytes 32768 | tf_op jit(solution)/shard_map/add | solution.py:19
  2.6 1.5 %copy.15 = s32[128,4,32]{0,1,2:T(4,128)} copy(s32[128,4,32]{0,2,1:T(8,128)} %param.7) | data formatting | bytes 131072 | tf_op args[1]
  4.2 3.1 %fusion.x_ref = bf16[32,128,128]{2,1,0:T(8,128)(2,1)} fusion(bf16[128,32,128]{2,1,0:T(8,128)(2,1)} %param.6, bf16[128,32]{0,1:T(8,128)(2,1)S(1)} %get-tuple-element.10, bf16[128,32]{0,1:T(8,128)(2,1)S(1)} %get-tuple-element.9), kind=kLoop, calls=%fused_computation.1 | loop fusion | flops 3145728 | bytes 2113536 | tf_op jit(solution)/shard_map/transpose | solution.py:450
  7.2 53.0 %shard_map.85 = (f32[2,1024,128]{2,1,0:T(8,128)}, f32[512,512]{1,0:T(8,128)}, f32[1,512]{1,0:T(1,128)}) custom-call(s32[32]{0:T(128)} %select_reduce_fusion.slot_ref, bf16[32,128,128]{2,1,0:T(8,128)(2,1)} %fusion.x_ref, s32[32,4,128]{2,1,0:T(4,128)} %bitcast.6, bf16[128,512]{1,0:T(8,128)(2,1)} %acts_ref.1, bf16[128,512]{1,0:T(8,128)(2,1)} %cot_ref.1), custom_call_target="tpu_custom_call" | custom-call | tf_op jit(solution)/shard_map/pallas_call | solution.py:463
  60.3 0.0 copy-start
  60.3 2.4 %copy.19 = f32[2,1024,128]{2,1,0:T(8,128)} copy(f32[2,1024,128]{2,1,0:T(8,128)} %get-tuple-element.14) | data formatting | bytes 2097152
  62.6 0.0 copy-done
  62.6 0.0 copy-start.1
  62.6 1.0 %copy.20 = f32[512,512]{1,0:T(8,128)} copy(f32[512,512]{1,0:T(8,128)S(1)} %copy-done) | data formatting | bytes 2097152
  63.6 0.0 copy-done.1
  63.6 0.6 copy.21
Async XLA Ops:
  60.3 2.4 %copy-start = (f32[512,512]{1,0:T(8,128)S(1)}, f32[512,512]{1,0:T(8,128)}, u32[]{:S(2)}) copy-start(f32[512,512]{1,0:T(8,128)} %get-tuple-element.15) | copy-start | bytes 3145732
  62.6 1.0 %copy-start.1 = (f32[1,512]{1,0:T(1,128)S(1)}, f32[1,512]{1,0:T(1,128)}, u32[]{:S(2)}) copy-start(f32[1,512]{1,0:T(1,128)} %get-tuple-element.8) | copy-start | bytes 6148
where the time goes:
time: 64.5 us; the launch traced here: 64.2 us
  Pallas kernels  53 us (82%)
  local copies, waits for them, and re-layouts  5.42 us (8%)
  other arithmetic  5.08 us (8%)
  between operations  0.65 us (1%)
    pallas_call x1, Pallas kernels, per_device(): pl.pallas_call(functools.partial(kernel, devs, pool), out_shape=(jax.Shap...  53 us
    unnamed x8, local copies, waits for them, and re-layouts  5.42 us
    transpose x1, other arithmetic, per_device(): jnp.transpose(jnp.clip(pooled_grad.astype(jnp.float32), -factor, factor)....  3.07 us

commit v1 on v0

v1 whole, which is shorter than its diff:
```python
import functools
import math

import jax
import jax.numpy as jnp
from jax import lax
from jax.experimental import pallas as pl
from jax.experimental.pallas import tpu as pltpu
from jax.sharding import PartitionSpec as P

ROWS = 1024
SPAN = 128
MESH = pl.DeviceIdType.MESH
CHUNKS = 4
PAD = 8
GROUP = 16
VMEM_MOST = 67043328
VMEM_SPARE = 8 << 20


def encode(ids):
    level = jnp.zeros(ids.shape, jnp.int32)
    scale = jnp.ones(ids.shape, jnp.float32)
    for k in range(1, ROWS // SPAN):
        level = jnp.where(ids >= k * SPAN, k, level)
        scale = jnp.where(ids >= k * SPAN, float(1 << k), scale)
    return (ids - level * SPAN + SPAN).astype(jnp.float32) * scale


def powers(exps):
    return (
        1.0
        + (exps >= 1).astype(jnp.float32)
        + 2.0 * (exps >= 2).astype(jnp.float32)
        + 4.0 * (exps >= 3).astype(jnp.float32)
    )


def kernel(
    devs,
    pool,
    owner_hbm,
    x_hbm,
    ids_hbm,
    exps_hbm,
    acts_hbm,
    cot_hbm,
    table_ref,
    whole,
    bias_ref,
    xv,
    xs,
    idv,
    exv,
    codes,
    base,
    owner_ref,
    slots,
    send,
    recv,
    inter,
    ga,
    gc,
    oa,
    oc,
    part,
    yh,
    zbuf,
    bp,
    bh,
    bz,
    bx,
    lsem,
    psend,
    precv,
    csend,
    crecv,
    fsend,
    frecv,
    isend,
    irecv,
    ysend,
    yrecv,
    zsend,
    zrecv,
    bsend,
    brecv,
    gsend,
    grecv,
    esend,
    erecv,
):
    me = lax.axis_index("dev")
    grp = lax.axis_index("grp")
    other = 1 - grp
    samples, tables, feat = x_hbm.shape
    owned = table_ref.shape[0]
    id_rows = owned * pool
    zs = devs // 4
    core = lax.rem(me, 2)
    xbit = lax.rem(lax.div(me, 2), 2)
    z = lax.div(me, 4)
    place = lax.rem(me, 4)
    tall, wide = oa.shape[1], oc.shape[1]
    cols = wide // 128
    half = part.shape[0] // 2
    piece = half // zs
    pitch = samples + PAD

    def remote(src, dst, ssem, rsem, dev, group):
        return pltpu.make_async_remote_copy(
            src_ref=src,
            dst_ref=dst,
            send_sem=ssem,
            recv_sem=rsem,
            device_id={"grp": group, "dev": dev},
            device_id_type=MESH,
        )

    places = (
        place,
        place + 1 - 2 * core,
        place + 2 - 4 * xbit,
        place + 3 - 4 * xbit - 2 * core,
    )
    near = z * 4 + places[1]
    across = z * 4 + places[2]

    def columns(ref, part_index, width):
        return ref.at[:, pl.ds(pl.multiple_of(part_index * width, 128), width)]

    def slot_rows(ref, index):
        return ref.at[pl.ds(pl.multiple_of(index * samples, 8), samples)]

    owner_load = pltpu.make_async_copy(owner_hbm, owner_ref, lsem.at[6 + CHUNKS])
    owner_load.start()
    loads = [
        pltpu.make_async_copy(columns(acts_hbm, core, tall), slot_rows(ga, place), lsem.at[0]),
        pltpu.make_async_copy(columns(cot_hbm, xbit, wide), slot_rows(gc, place), lsem.at[1]),
        pltpu.make_async_copy(columns(acts_hbm, 1 - core, tall), oa, lsem.at[2]),
        pltpu.make_async_copy(columns(cot_hbm, 1 - xbit, wide), oc, lsem.at[3]),
        pltpu.make_async_copy(exps_hbm, exv, lsem.at[4]),
        pltpu.make_async_copy(ids_hbm, idv, lsem.at[5]),
    ]
    step = samples // CHUNKS
    for c in range(CHUNKS):
        span = pl.ds(c * step, step)
        loads.append(pltpu.make_async_copy(x_hbm.at[span], xv.at[span], lsem.at[6 + c]))
    for load in loads:
        load.start()

    barrier = pltpu.get_barrier_semaphore()

    def greet(dev, group):
        pl.semaphore_signal(
            barrier, inc=1, device_id={"grp": group, "dev": dev}, device_id_type=MESH
        )

    for m in range(1, 4):
        greet(z * 4 + places[m], grp)

    @pl.loop(1, zs)
    def _(k):
        greet(lax.rem(z + k, zs) * 4 + place, grp)

    greet(me, other)

    base[...] = (
        (lax.broadcasted_iota(jnp.int32, base.shape, 0) + SPAN)
        .astype(jnp.float32)
        .astype(jnp.bfloat16)
    )

    owner_load.wait()

    @pl.loop(0, tables)
    def _(k):
        slots[k] = lax.fori_loop(
            0,
            tables,
            lambda t, found: jnp.maximum(found, (owner_ref[t] == k).astype(jnp.int32) * t),
            jnp.int32(0),
            unroll=16,
        )

    pl.semaphore_wait(barrier, 3 + zs)

    def plane_copies(m, slot):
        acts = oa if m in (1, 3) else slot_rows(ga, place)
        cots = oc if m in (2, 3) else slot_rows(gc, place)
        who = z * 4 + places[m]
        return (
            remote(
                acts, slot_rows(ga, slot), isend.at[2 * m - 2], irecv.at[2 * m - 2], who, grp
            ),
            remote(
                cots, slot_rows(gc, slot), isend.at[2 * m - 1], irecv.at[2 * m - 1], who, grp
            ),
        )

    for load in loads[:4]:
        load.wait()
    for m in (2, 3, 1):
        for copy in plane_copies(m, place):
            copy.start()

    loads[4].wait()
    loads[5].wait()
    for p in range(pool):
        codes.reshape(tables * 8, samples)[pl.ds(p, tables, stride=8), :] = encode(idv[p])

    flat = xs.reshape(tables * pitch, feat)
    for c in range(CHUNKS):
        loads[6 + c].wait()

        @pl.loop(0, tables // GROUP)
        def _(g):
            some = pl.ds(pl.multiple_of(g * GROUP, GROUP), GROUP)
            factor = powers(exv[some, :])
            first = g * (GROUP * pitch)
            for k in range(c * step, (c + 1) * step):
                bound = jnp.broadcast_to(factor[:, k : k + 1], (GROUP, feat))
                value = xv[k, some, :].astype(jnp.float32)
                rows = pl.ds(first + k, GROUP, stride=pitch)
                flat[rows, :] = jnp.clip(value, -bound, bound)

    def build(target, dst):
        picked = []
        for s in range(owned):
            t = slots[dst * owned + s]
            target[pl.ds(s * samples, samples), :] = xs[t][:samples].astype(jnp.bfloat16)
            picked.append(codes[t][:pool])
        target[pl.ds(owned * samples, id_rows), :] = jnp.concatenate(picked, axis=0).astype(
            jnp.bfloat16
        )

    def each_far(act):
        @pl.loop(1, zs)
        def _(i):
            for peer in (z + zs - i, z - zs + i):
                pl.when((peer >= 0) & (peer < zs))(functools.partial(act, peer))

    def each_near(act):
        @pl.loop(1, zs)
        def _(i):
            for peer in (z + i, z - i):
                pl.when((peer >= 0) & (peer < zs))(functools.partial(act, peer))

    def column_copy(m, peer):
        return remote(
            send.at[peer * 4 + places[m]],
            inter.at[m - 1, peer],
            psend.at[m - 1, peer],
            precv.at[m - 1, peer],
            z * 4 + places[m],
            grp,
        )

    def level_copy(m, back=False):
        who = z * 4 + places[m]
        return remote(
            send.at[who],
            recv.at[0, who if back else me],
            psend.at[m - 1, z],
            precv.at[m - 1, z],
            who,
            grp,
        )

    def line_copy(m, peer):
        origin = send.at[peer * 4 + place] if m == 0 else inter.at[m - 1, peer]
        return remote(
            origin,
            recv.at[0, z * 4 + places[m]],
            csend.at[m, peer],
            crecv.at[m, z],
            peer * 4 + place,
            grp,
        )

    def line_wait(m, peer):
        landing = recv.at[0, peer * 4 + places[m]]
        remote(
            landing, landing, csend.at[m, peer], crecv.at[m, peer], peer * 4 + place, grp
        ).wait_recv()

    def forward(src):
        return remote(
            recv.at[0, src], recv.at[1, src], fsend.at[src], frecv.at[src], me, other
        )

    def first_line(peer):
        dst = peer * 4 + place
        build(send.at[dst], dst)
        line_copy(0, peer).start()

    def column_start(m):
        def act(peer):
            dst = peer * 4 + places[m]
            build(send.at[dst], dst)
            column_copy(m, peer).start()

        each_far(act)
        build(send.at[z * 4 + places[m]], z * 4 + places[m])
        level_copy(m).start()

    def column_pass(m):
        def act(peer):
            column_copy(m, peer).wait_recv()
            line_copy(m, peer).start()

        each_far(act)

    def level_pass(m):
        level_copy(m, True).wait_recv()
        forward(z * 4 + places[m]).start()

    def line_pass(m):
        def act(peer):
            line_wait(m, peer)
            forward(peer * 4 + places[m]).start()

        each_near(act)

    def plane_finish():
        for m in range(1, 4):
            for copy in plane_copies(m, places[m]):
                copy.wait_recv()
        grad = lax.dot_general(
            ga[...], gc[...], (((0,), (0,)), ((), ())), preferred_element_type=jnp.float32
        )
        bias = jnp.sum(gc[...].astype(jnp.float32), axis=0, keepdims=True)
        bp[0] = jnp.zeros(bp.shape[1:], jnp.float32)
        for j in range(cols):
            part[pl.ds(j * tall, tall), :] = grad[:, j * 128 : (j + 1) * 128]
            bp[0, j : j + 1, :] = bias[:, j * 128 : (j + 1) * 128]

    def y_copies():
        away = part.at[pl.ds(pl.multiple_of(other * half, 8), half)]
        return (
            remote(away, yh, ysend.at[0], yrecv.at[0], me, other),
            remote(bp.at[0], bh, ysend.at[1], yrecv.at[1], me, other),
        )

    def y_start():
        for copy in y_copies():
            copy.start()

    def y_finish():
        for copy in y_copies():
            copy.wait()
        keep = pl.ds(pl.multiple_of(grp * half, 8), half)
        part[keep, :] = part[keep, :] + yh[...]
        bp[1] = bp[0] + bh[...]

    def piece_of(peer):
        return pl.ds(pl.multiple_of(grp * half + peer * piece, 8), piece)

    def z_copy(k, back=False):
        peer = lax.rem(z + k, zs)
        dev = peer * 4 + place
        origin, landing = (z, peer) if back else (peer, z)
        return (
            remote(
                part.at[piece_of(origin)],
                zbuf.at[landing],
                zsend.at[peer],
                zrecv.at[landing],
                dev,
                grp,
            ),
            remote(bp.at[1], bz.at[landing], bsend.at[peer], brecv.at[landing], dev, grp),
        )

    def z_start():
        @pl.loop(1, zs)
        def _(k):
            for copy in z_copy(k):
                copy.start()

    def z_finish():
        zbuf[z] = part[piece_of(z), :]
        bz[z] = bp[1]

        @pl.loop(1, zs)
        def _(k):
            for copy in z_copy(k, True):
                copy.wait_recv()

        whole[place, piece_of(z), :] = lax.fori_loop(
            1, zs, lambda i, run: run + zbuf[i], zbuf[0]
        )
        bp[2] = lax.fori_loop(1, zs, lambda i, run: run + bz[i], bz[0])

    def zg_copy(k, back=False):
        peer = lax.rem(z + k, zs)
        block = whole.at[place, piece_of(peer if back else z)]
        return remote(
            block, block, gsend.at[peer], grecv.at[peer if back else z], peer * 4 + place, grp
        )

    def bias_copy():
        return remote(bp.at[2], bx, bsend.at[zs], brecv.at[zs], across, grp)

    def zg_start():
        @pl.loop(1, zs)
        def _(k):
            zg_copy(k).start()

        bias_copy().start()

    def zg_finish():
        @pl.loop(1, zs)
        def _(k):
            zg_copy(k, True).wait_recv()

    halves = (grp, other)

    def tile_half(tile, which):
        return whole.at[tile, pl.ds(pl.multiple_of(which * half, 8), half)]

    def gather_copy(k, back=False):
        if k == 0:
            block = tile_half(place, other if back else grp)
            return remote(block, block, esend.at[0], erecv.at[0], me, other)
        if k < 3:
            block = tile_half(places[2] if back else place, halves[k - 1])
            return remote(block, block, esend.at[k], erecv.at[k], across, grp)
        if k < 5:
            block = tile_half(places[1] if back else place, halves[k - 3])
        else:
            block = tile_half(places[3] if back else places[2], halves[k - 5])
        return remote(block, block, esend.at[k], erecv.at[k], near, grp)

    def gather_start(*ks):
        for k in ks:
            gather_copy(k).start()

    def gather_wait(*ks):
        for k in ks:
            gather_copy(k, True).wait_recv()

    def accumulate(side, first, second):
        marks = jnp.concatenate(
            [
                recv[side, c, pl.ds(owned * samples, id_rows), :].astype(jnp.float32)
                for c in (first, second)
            ],
            axis=1,
        )
        one, zero = jnp.bfloat16(1), jnp.bfloat16(0)
        axis = base[...]
        for s in range(owned):
            values = jnp.concatenate(
                [recv[side, c, pl.ds(s * samples, samples), :] for c in (first, second)],
                axis=0,
            )
            rows = marks[s * pool : (s + 1) * pool]
            for block in range(ROWS // SPAN):
                local = (rows * (1.0 / (1 << block))).astype(jnp.bfloat16)
                counts = jnp.where(local[0:1] == axis, one, zero)
                for p in range(1, pool):
                    counts = counts + jnp.where(local[p : p + 1] == axis, one, zero)
                span = pl.ds(block * SPAN, SPAN)
                table_ref[s, span, :] = table_ref[s, span, :] + jnp.dot(
                    counts, values, preferred_element_type=jnp.float32
                )

    def pair(side, part_of, peer):
        accumulate(side, peer * 4 + places[2 * part_of], peer * 4 + places[2 * part_of + 1])

    def own_pairs(part_of):
        pair(0, part_of, z)
        each_near(functools.partial(pair, 0, part_of))

    def far_pair(part_of, peer):
        for m in (2 * part_of, 2 * part_of + 1):
            forward(peer * 4 + places[m]).wait_recv()
        pair(1, part_of, peer)

    each_far(first_line)
    build(recv.at[0, me], me)
    forward(me).start()
    column_start(1)
    column_start(2)
    column_start(3)
    column_pass(1)
    level_pass(1)
    table_ref[...] = jnp.zeros(table_ref.shape, jnp.float32)

    plane_finish()
    y_start()
    line_pass(0)
    y_finish()
    z_start()
    column_pass(2)
    level_pass(2)
    pair(0, 0, z)
    line_pass(1)
    z_finish()
    zg_start()
    column_pass(3)
    level_pass(3)
    each_near(functools.partial(pair, 0, 0))
    far_pair(0, z)
    line_pass(2)
    zg_finish()
    gather_start(0, 1, 3)
    pair(0, 1, z)
    each_near(functools.partial(far_pair, 0))
    gather_wait(0)
    gather_start(2, 4)
    line_pass(3)
    each_near(functools.partial(pair, 0, 1))
    gather_wait(1)
    gather_start(5)
    far_pair(1, z)
    gather_wait(2)
    gather_start(6)
    each_near(functools.partial(far_pair, 1))
    gather_wait(3, 4, 5, 6)


    bias_copy().wait_recv()
    mine, theirs = bp[2], bx[...]
    lower = jnp.where(xbit == 0, mine, theirs)
    upper = jnp.where(xbit == 0, theirs, mine)
    for j in range(cols):
        bias_ref[:, j * 128 : (j + 1) * 128] = lower[j : j + 1, :]
        bias_ref[:, (cols + j) * 128 : (cols + j + 1) * 128] = upper[j : j + 1, :]

    bias_copy().wait_send()
    for k in range(7):
        gather_copy(k).wait_send()
    for m in range(1, 4):
        level_copy(m).wait_send()
        for copy in plane_copies(m, place):
            copy.wait_send()

    @pl.loop(1, zs)
    def _(k):
        for copy in z_copy(k):
            copy.wait_send()
        zg_copy(k).wait_send()

    def drain(peer):
        for m in range(4):
            line_copy(m, peer).wait_send()
            if m > 0:
                column_copy(m, peer).wait_send()

    each_near(drain)

    @pl.loop(0, devs)
    def _(src):
        forward(src).wait_send()


def place_outputs(table_in, whole_in, bias_in, table_out, weight_out, bias_out, sems):
    tiles, rows, _ = whole_in.shape
    tall = weight_out.shape[0] // 2
    cols = rows // tall
    copies = []
    for s in range(table_in.shape[0]):
        copies.append((table_in.at[s], table_out.at[s]))
    for tile in range(tiles):
        for j in range(cols):
            block = (tile // 2) * cols + j
            copies.append(
                (
                    whole_in.at[tile, pl.ds(j * tall, tall)],
                    weight_out.at[pl.ds((tile % 2) * tall, tall), pl.ds(block * 128, 128)],
                )
            )
    copies.append((bias_in, bias_out))
    started = [
        pltpu.make_async_copy(src, dst, sems.at[i]) for i, (src, dst) in enumerate(copies)
    ]
    for copy in started:
        copy.start()
    for copy in started:
        copy.wait()


def solution(mesh):
    devs = mesh.shape["dev"]

    def per_device(pooled_grad, row_ids, scale_exps, table_owner, dense_acts, dense_cot):
        samples, tables, feat = pooled_grad.shape
        pool = row_ids.shape[1]
        owned = tables // devs
        hid, hid2 = dense_acts.shape[1], dense_cot.shape[1]
        tall, wide = hid // 2, hid2 // 2
        zs = devs // 4
        rows = owned * (samples + pool)
        total = tall * wide // 128
        half = total // 2
        dma = pltpu.SemaphoreType.DMA
        vmem = pl.BlockSpec(memory_space=pltpu.VMEM)
        hbm = pl.BlockSpec(memory_space=pltpu.HBM)
        f32, bf16, i32 = jnp.float32, jnp.bfloat16, jnp.int32
        buffers = [
            pltpu.VMEM((samples, tables, feat), bf16),
            pltpu.VMEM((tables, samples + PAD, feat), f32),
            pltpu.VMEM((pool, tables, samples), i32),
            pltpu.VMEM((tables, samples), i32),
            pltpu.VMEM((tables, 8, samples), f32),
            pltpu.VMEM((SPAN, 2 * samples), bf16),
            pltpu.VMEM((devs, rows, feat), bf16),
            pltpu.VMEM((2, devs, rows, feat), bf16),
            pltpu.VMEM((3, zs, rows, feat), bf16),
            pltpu.VMEM((4 * samples, tall), bf16),
            pltpu.VMEM((4 * samples, wide), bf16),
            pltpu.VMEM((samples, tall), bf16),
            pltpu.VMEM((samples, wide), bf16),
            pltpu.VMEM((total, 128), f32),
            pltpu.VMEM((half, 128), f32),
            pltpu.VMEM((zs, half // zs, 128), f32),
            pltpu.VMEM((3, 8, 128), f32),
            pltpu.VMEM((8, 128), f32),
            pltpu.VMEM((zs, 8, 128), f32),
            pltpu.VMEM((8, 128), f32),
        ]
        held = sum(math.prod(b.shape) * jnp.dtype(b.dtype).itemsize for b in buffers)
        partial = pl.pallas_call(
            functools.partial(kernel, devs, pool),
            out_shape=(
                jax.ShapeDtypeStruct((owned, ROWS, feat), f32),
                jax.ShapeDtypeStruct((4, total, 128), f32),
                jax.ShapeDtypeStruct((1, hid2), f32),
            ),
            in_specs=[hbm] * 6,
            out_specs=(vmem, vmem, vmem),
            scratch_shapes=buffers[:6]
            + [pltpu.SMEM((tables,), i32)] * 2
            + buffers[6:]
            + [
                dma((7 + CHUNKS,)),
                dma((3, zs)),
                dma((3, zs)),
                dma((4, zs)),
                dma((4, zs)),
                dma((devs,)),
                dma((devs,)),
                dma((6,)),
                dma((6,)),
                dma((2,)),
                dma((2,)),
                dma((zs,)),
                dma((zs,)),
                dma((zs + 1,)),
                dma((zs + 1,)),
                dma((zs,)),
                dma((zs,)),
                dma((7,)),
                dma((7,)),
            ],
            compiler_params=pltpu.CompilerParams(
                collective_id=0,
                has_side_effects=True,
                vmem_limit_bytes=min(held + VMEM_SPARE, VMEM_MOST),
            ),
        )(
            pltpu.with_memory_space_constraint(table_owner, pltpu.HBM),
            pltpu.with_memory_space_constraint(pooled_grad, pltpu.HBM),
            pltpu.with_memory_space_constraint(jnp.transpose(row_ids, (1, 2, 0)), pltpu.HBM),
            pltpu.with_memory_space_constraint(jnp.transpose(scale_exps, (1, 0)), pltpu.HBM),
            pltpu.with_memory_space_constraint(dense_acts, pltpu.HBM),
            pltpu.with_memory_space_constraint(dense_cot, pltpu.HBM),
        )
        cols = total // tall
        table_grad, weight_grad, bias_grad = pl.pallas_call(
            place_outputs,
            out_shape=(
                jax.ShapeDtypeStruct((owned, ROWS, feat), f32),
                jax.ShapeDtypeStruct((hid, hid2), f32),
                jax.ShapeDtypeStruct((1, hid2), f32),
            ),
            in_specs=[vmem] * 3,
            out_specs=(hbm, hbm, hbm),
            scratch_shapes=[dma((owned + 4 * cols + 1,))],
            compiler_params=pltpu.CompilerParams(vmem_limit_bytes=16 << 20),
        )(*partial)
        return table_grad, weight_grad, bias_grad.reshape(hid2)

    return jax.shard_map(
        per_device,
        mesh=mesh,
        in_specs=(
            P(("grp", "dev"), None, None),
            P(("grp", "dev"), None, None),
            P(("grp", "dev"), None),
            P(),
            P(("grp", "dev"), None),
            P(("grp", "dev"), None),
        ),
        out_specs=(P("dev", None, None), P(), P()),
        check_vma=False,
    )
```

time: 64.5 us -> 52.1 us (0.81)
  local copies, waits for them, and re-layouts: 5.42 us -> 0 us
  other arithmetic: 5.08 us -> 0 us
  Pallas kernels: 53 us -> 51.3 us
    unnamed x8 -> x0, local copies, waits for them, and re-layouts: 5.42 us -> none
    pallas_call x1, Pallas kernels: 53 us -> 49.9 us  [per_device(): pl.pallas_call(functools.partial(kernel, devs, pool), out_shape=(jax.Shap...]
    transpose x1 -> x0, other arithmetic: 3.07 us -> none  [per_device(): jnp.transpose(jnp.clip(pooled_grad.astype(jnp.float32), -factor, factor)....]
    pallas_call x0 -> x1, Pallas kernels: none -> 1.4 us  [per_device(): pl.pallas_call(place_outputs, out_shape=(jax.ShapeDtypeStruct((owned, ROW...]
    reduce_sum x1 -> x0, other arithmetic: 1.28 us -> none  [per_device(): jnp.sum(jnp.where(table_owner[None, :] == order[:, None], order[None, :],...]
    add x1 -> x0, other arithmetic: 0.73 us -> none  [powers(): 1.0 + (exps >= 1).astype(jnp.float32)]
where the time goes in v1:
time: 52.1 us; the launch traced here: 52 us
  Pallas kernels  51.3 us (98%)
  between operations  0.64 us (1%)
    pallas_call x1, Pallas kernels, per_device(): pl.pallas_call(functools.partial(kernel, devs, pool), out_shape=(jax.Shap...  49.9 us
    pallas_call x1, Pallas kernels, per_device(): pl.pallas_call(place_outputs, out_shape=(jax.ShapeDtypeStruct((owned, ROW...  1.4 us

profile of v1, /device:TPU:0, one launch (start us, length us, event | category | flops | bytes accessed | tf_op | source)
XLA Modules:
  0.0 52.0 jit_solution(12257798240608569644)
XLA Ops:
  0.6 49.9 %shard_map.85 = (f32[2,1024,128]{2,1,0:T(8,128)S(1)}, f32[4,512,128]{2,1,0:T(8,128)S(1)}, f32[1,512]{1,0:T(1,128)S(1)}) custom-call(s32[32]{0:T(128)} %owner_hbm.1, bf16[128,32,128]{2,1,0:T(8,128)(2,1)} %x_hbm.1, s32[4,32,128]{2,1,0:T(8,128)} %bitcast.3, s32[32,128]{1,0:T(8,128)} %bitcast.4, bf16[128,512]{1,0:T(8,128)(2,1)} %acts_hbm.1, bf16[128,512]{1,0:T(8,128)(2,1)} %cot_hbm.1), custom_call_target="tpu_custom_call" | custom-call | tf_op jit(solution)/shard_map/pallas_call | solution.py:625
  50.6 1.4 %shard_map.86 = (f32[2,1024,128]{2,1,0:T(8,128)}, f32[512,512]{1,0:T(8,128)}, f32[1,512]{1,0:T(1,128)}) custom-call(f32[2,1024,128]{2,1,0:T(8,128)S(1)} %get-tuple-element.9.table_in, f32[4,512,128]{2,1,0:T(8,128)S(1)} %get-tuple-element.10.whole_in, f32[1,512]{1,0:T(1,128)S(1)} %get-tuple-element.11.bias_in), custom_call_target="tpu_custom_call" | custom-call | tf_op jit(solution)/shard_map/pallas_call | solution.py:672

commit v2 on v1

--- a/solution.py
+++ b/solution.py
@@ -234,17 +234,19 @@
             jnp.bfloat16
         )
 
-    def each_far(act):
-        @pl.loop(1, zs)
+    def each_near(act, first=1, last=zs):
+        @pl.loop(first, last)
         def _(i):
-            for peer in (z + zs - i, z - zs + i):
+            @pl.loop(0, 2)
+            def _(j):
+                peer = z + i * (1 - 2 * j)
                 pl.when((peer >= 0) & (peer < zs))(functools.partial(act, peer))
 
-    def each_near(act):
-        @pl.loop(1, zs)
-        def _(i):
-            for peer in (z + i, z - i):
-                pl.when((peer >= 0) & (peer < zs))(functools.partial(act, peer))
+    def close(act):
+        each_near(act, 1, 2)
+
+    def rest(act):
+        each_near(act, 2, zs)
 
     def column_copy(m, peer):
         return remote(
@@ -300,27 +302,29 @@
             build(send.at[dst], dst)
             column_copy(m, peer).start()
 
-        each_far(act)
+        each_near(act)
+
+    def level_start(m):
         build(send.at[z * 4 + places[m]], z * 4 + places[m])
         level_copy(m).start()
 
-    def column_pass(m):
+    def column_pass(m, each):
         def act(peer):
             column_copy(m, peer).wait_recv()
             line_copy(m, peer).start()
 
-        each_far(act)
+        each(act)
 
     def level_pass(m):
         level_copy(m, True).wait_recv()
         forward(z * 4 + places[m]).start()
 
-    def line_pass(m):
+    def line_pass(m, each):
         def act(peer):
             line_wait(m, peer)
             forward(peer * 4 + places[m]).start()
 
-        each_near(act)
+        each(act)
 
     def plane_finish():
         for m in range(1, 4):
@@ -469,57 +473,66 @@
     def pair(side, part_of, peer):
         accumulate(side, peer * 4 + places[2 * part_of], peer * 4 + places[2 * part_of + 1])
 
-    def own_pairs(part_of):
-        pair(0, part_of, z)
-        each_near(functools.partial(pair, 0, part_of))
-
     def far_pair(part_of, peer):
         for m in (2 * part_of, 2 * part_of + 1):
             forward(peer * 4 + places[m]).wait_recv()
         pair(1, part_of, peer)
 
-    each_far(first_line)
+    each_near(first_line)
     build(recv.at[0, me], me)
     forward(me).start()
+    level_start(1)
+    level_start(2)
+    level_start(3)
     column_start(1)
     column_start(2)
     column_start(3)
-    column_pass(1)
+    column_pass(1, close)
+    column_pass(1, rest)
     level_pass(1)
     table_ref[...] = jnp.zeros(table_ref.shape, jnp.float32)
-
     plane_finish()
     y_start()
-    line_pass(0)
+    line_pass(0, close)
     y_finish()
     z_start()
-    column_pass(2)
     level_pass(2)
+    level_pass(3)
+    line_pass(0, rest)
+    column_pass(2, close)
     pair(0, 0, z)
-    line_pass(1)
+    line_pass(1, close)
     z_finish()
     zg_start()
-    column_pass(3)
-    level_pass(3)
-    each_near(functools.partial(pair, 0, 0))
+    column_pass(2, rest)
+    line_pass(1, rest)
+    column_pass(3, close)
+    column_pass(3, rest)
+    close(functools.partial(pair, 0, 0))
+    rest(functools.partial(pair, 0, 0))
     far_pair(0, z)
-    line_pass(2)
+    line_pass(2, close)
     zg_finish()
     gather_start(0, 1, 3)
+    line_pass(2, rest)
     pair(0, 1, z)
-    each_near(functools.partial(far_pair, 0))
+    close(functools.partial(far_pair, 0))
+    rest(functools.partial(far_pair, 0))
     gather_wait(0)
     gather_start(2, 4)
-    line_pass(3)
-    each_near(functools.partial(pair, 0, 1))
+    line_pass(3, close)
+    line_pass(3, rest)
+    close(functools.partial(pair, 0, 1))
+    rest(functools.partial(pair, 0, 1))
     gather_wait(1)
     gather_start(5)
     far_pair(1, z)
     gather_wait(2)
     gather_start(6)
-    each_near(functools.partial(far_pair, 1))
-    gather_wait(3, 4, 5, 6)
-
+    close(functools.partial(far_pair, 1))
+    rest(functools.partial(far_pair, 1))
+    gather_wait(3, 4)
+    gather_wait(5, 6)
 
     bias_copy().wait_recv()
     mine, theirs = bp[2], bx[...]

time: 52.1 us -> 49.8 us (0.956)
  Pallas kernels: 51.3 us -> 49 us
    pallas_call x1, Pallas kernels: 49.9 us -> 47.6 us  [per_device(): pl.pallas_call(functools.partial(kernel, devs, pool), out_shape=(jax.Shap...]
where the time goes in v2:
time: 49.8 us; the launch traced here: 49.7 us
  Pallas kernels  49 us (98%)
  between operations  0.64 us (1%)
    pallas_call x1, Pallas kernels, per_device(): pl.pallas_call(functools.partial(kernel, devs, pool), out_shape=(jax.Shap...  47.6 us
    pallas_call x1, Pallas kernels, per_device(): pl.pallas_call(place_outputs, out_shape=(jax.ShapeDtypeStruct((owned, ROW...  1.4 us

profile of v2, /device:TPU:0, one launch (start us, length us, event | category | flops | bytes accessed | tf_op | source)
XLA Modules:
  0.0 49.7 jit_solution(9463106557514777910)
XLA Ops:
  0.6 47.6 %shard_map.85 = (f32[2,1024,128]{2,1,0:T(8,128)S(1)}, f32[4,512,128]{2,1,0:T(8,128)S(1)}, f32[1,512]{1,0:T(1,128)S(1)}) custom-call(s32[32]{0:T(128)} %owner_hbm.1, bf16[128,32,128]{2,1,0:T(8,128)(2,1)} %x_hbm.1, s32[4,32,128]{2,1,0:T(8,128)} %bitcast.3, s32[32,128]{1,0:T(8,128)} %bitcast.4, bf16[128,512]{1,0:T(8,128)(2,1)} %acts_hbm.1, bf16[128,512]{1,0:T(8,128)(2,1)} %cot_hbm.1), custom_call_target="tpu_custom_call" | custom-call | tf_op jit(solution)/shard_map/pallas_call | solution.py:638
  48.3 1.4 %shard_map.86 = (f32[2,1024,128]{2,1,0:T(8,128)}, f32[512,512]{1,0:T(8,128)}, f32[1,512]{1,0:T(1,128)}) custom-call(f32[2,1024,128]{2,1,0:T(8,128)S(1)} %get-tuple-element.9.table_in, f32[4,512,128]{2,1,0:T(8,128)S(1)} %get-tuple-element.10.whole_in, f32[1,512]{1,0:T(1,128)S(1)} %get-tuple-element.11.bias_in), custom_call_target="tpu_custom_call" | custom-call | tf_op jit(solution)/shard_map/pallas_call | solution.py:685

commit v3 on v2

--- a/solution.py
+++ b/solution.py
@@ -14,6 +14,8 @@
 CHUNKS = 4
 PAD = 8
 GROUP = 16
+LEVELS = 32767.0
+TINY = 1e-30
 VMEM_MOST = 67043328
 VMEM_SPARE = 8 << 20
 
@@ -70,6 +72,8 @@
     bh,
     bz,
     bx,
+    coded,
+    steps,
     lsem,
     psend,
     precv,
@@ -330,14 +334,22 @@
         for m in range(1, 4):
             for copy in plane_copies(m, places[m]):
                 copy.wait_recv()
-        grad = lax.dot_general(
-            ga[...], gc[...], (((0,), (0,)), ((), ())), preferred_element_type=jnp.float32
-        )
         bias = jnp.sum(gc[...].astype(jnp.float32), axis=0, keepdims=True)
         bp[0] = jnp.zeros(bp.shape[1:], jnp.float32)
         for j in range(cols):
-            part[pl.ds(j * tall, tall), :] = grad[:, j * 128 : (j + 1) * 128]
             bp[0, j : j + 1, :] = bias[:, j * 128 : (j + 1) * 128]
+        each = cols // 2
+        for which in (other, grp):
+            for j in range(each):
+                block = which * each + j
+                part[pl.ds(pl.multiple_of(block * tall, 8), tall), :] = lax.dot_general(
+                    ga[...],
+                    gc[:, pl.ds(pl.multiple_of(block * 128, 128), 128)],
+                    (((0,), (0,)), ((), ())),
+                    preferred_element_type=jnp.float32,
+                )
+            if which is other:
+                y_start()
 
     def y_copies():
         away = part.at[pl.ds(pl.multiple_of(other * half, 8), half)]
@@ -352,7 +364,7 @@
 
     def y_finish():
         for copy in y_copies():
-            copy.wait()
+            copy.wait_recv()
         keep = pl.ds(pl.multiple_of(grp * half, 8), half)
         part[keep, :] = part[keep, :] + yh[...]
         bp[1] = bp[0] + bh[...]
@@ -391,17 +403,25 @@
             for copy in z_copy(k, True):
                 copy.wait_recv()
 
-        whole[place, piece_of(z), :] = lax.fori_loop(
-            1, zs, lambda i, run: run + zbuf[i], zbuf[0]
-        )
+        total = lax.fori_loop(1, zs, lambda i, run: run + zbuf[i], zbuf[0])
+        total = total.reshape(piece // 8, 8, 128)
+        top = jnp.maximum(jnp.max(jnp.abs(total), axis=0), TINY)
+        code = jnp.round(total * (LEVELS / top)).astype(jnp.int32)
+        coded[place, grp, z] = code.reshape(piece, 128).astype(jnp.int16)
+        steps[place, grp, z] = top * (1.0 / LEVELS)
         bp[2] = lax.fori_loop(1, zs, lambda i, run: run + bz[i], bz[0])
 
     def zg_copy(k, back=False):
         peer = lax.rem(z + k, zs)
-        block = whole.at[place, piece_of(peer if back else z)]
-        return remote(
-            block, block, gsend.at[peer], grecv.at[peer if back else z], peer * 4 + place, grp
-        )
+        dev = peer * 4 + place
+        origin = peer if back else z
+        return [
+            remote(ref.at[place, grp, origin], ref.at[place, grp, origin], ss, rs, dev, grp)
+            for ref, ss, rs in (
+                (coded, gsend.at[0, peer], grecv.at[0, origin]),
+                (steps, gsend.at[1, peer], grecv.at[1, origin]),
+            )
+        ]
 
     def bias_copy():
         return remote(bp.at[2], bx, bsend.at[zs], brecv.at[zs], across, grp)
@@ -409,40 +429,53 @@
     def zg_start():
         @pl.loop(1, zs)
         def _(k):
-            zg_copy(k).start()
+            for copy in zg_copy(k):
+                copy.start()
 
         bias_copy().start()
 
     def zg_finish():
         @pl.loop(1, zs)
         def _(k):
-            zg_copy(k, True).wait_recv()
+            for copy in zg_copy(k, True):
+                copy.wait_recv()
 
     halves = (grp, other)
-
-    def tile_half(tile, which):
-        return whole.at[tile, pl.ds(pl.multiple_of(which * half, 8), half)]
 
     def gather_copy(k, back=False):
         if k == 0:
-            block = tile_half(place, other if back else grp)
-            return remote(block, block, esend.at[0], erecv.at[0], me, other)
-        if k < 3:
-            block = tile_half(places[2] if back else place, halves[k - 1])
-            return remote(block, block, esend.at[k], erecv.at[k], across, grp)
-        if k < 5:
-            block = tile_half(places[1] if back else place, halves[k - 3])
+            tile, which, dev, group = place, other if back else grp, me, other
+        elif k < 3:
+            tile, which, dev, group = places[2] if back else place, halves[k - 1], across, grp
+        elif k < 5:
+            tile, which, dev, group = places[1] if back else place, halves[k - 3], near, grp
         else:
-            block = tile_half(places[3] if back else places[2], halves[k - 5])
-        return remote(block, block, esend.at[k], erecv.at[k], near, grp)
+            tile = places[3] if back else places[2]
+            which, dev, group = halves[k - 5], near, grp
+        return [
+            remote(
+                ref.at[tile, which], ref.at[tile, which], esend.at[i, k], erecv.at[i, k], dev, group
+            )
+            for i, ref in enumerate((coded, steps))
+        ]
 
     def gather_start(*ks):
         for k in ks:
-            gather_copy(k).start()
+            for copy in gather_copy(k):
+                copy.start()
 
     def gather_wait(*ks):
         for k in ks:
-            gather_copy(k, True).wait_recv()
+            for copy in gather_copy(k, True):
+                copy.wait_recv()
+
+    def decode(tile, which):
+        @pl.loop(0, zs)
+        def _(i):
+            code = coded[tile, which, i].astype(jnp.int32).astype(jnp.float32)
+            value = code.reshape(piece // 8, 8, 128) * steps[tile, which, i]
+            rows = pl.ds(pl.multiple_of(which * half + i * piece, 8), piece)
+            whole[tile, rows, :] = value.reshape(piece, 128)
 
     def accumulate(side, first, second):
         marks = jnp.concatenate(
@@ -492,7 +525,6 @@
     level_pass(1)
     table_ref[...] = jnp.zeros(table_ref.shape, jnp.float32)
     plane_finish()
-    y_start()
     line_pass(0, close)
     y_finish()
     z_start()
@@ -520,19 +552,27 @@
     rest(functools.partial(far_pair, 0))
     gather_wait(0)
     gather_start(2, 4)
+    decode(place, grp)
+    decode(place, other)
     line_pass(3, close)
     line_pass(3, rest)
     close(functools.partial(pair, 0, 1))
     rest(functools.partial(pair, 0, 1))
     gather_wait(1)
     gather_start(5)
+    decode(places[2], grp)
     far_pair(1, z)
     gather_wait(2)
     gather_start(6)
+    decode(places[2], other)
     close(functools.partial(far_pair, 1))
     rest(functools.partial(far_pair, 1))
     gather_wait(3, 4)
+    decode(places[1], grp)
+    decode(places[1], other)
     gather_wait(5, 6)
+    decode(places[3], grp)
+    decode(places[3], other)
 
     bias_copy().wait_recv()
     mine, theirs = bp[2], bx[...]
@@ -543,8 +583,11 @@
         bias_ref[:, (cols + j) * 128 : (cols + j + 1) * 128] = upper[j : j + 1, :]
 
     bias_copy().wait_send()
+    for copy in y_copies():
+        copy.wait_send()
     for k in range(7):
-        gather_copy(k).wait_send()
+        for copy in gather_copy(k):
+            copy.wait_send()
     for m in range(1, 4):
         level_copy(m).wait_send()
         for copy in plane_copies(m, place):
@@ -554,7 +597,8 @@
     def _(k):
         for copy in z_copy(k):
             copy.wait_send()
-        zg_copy(k).wait_send()
+        for copy in zg_copy(k):
+            copy.wait_send()
 
     def drain(peer):
         for m in range(4):
@@ -633,6 +677,8 @@
             pltpu.VMEM((8, 128), f32),
             pltpu.VMEM((zs, 8, 128), f32),
             pltpu.VMEM((8, 128), f32),
+            pltpu.VMEM((4, 2, zs, half // zs, 128), jnp.int16),
+            pltpu.VMEM((4, 2, zs, 8, 128), f32),
         ]
         held = sum(math.prod(b.shape) * jnp.dtype(b.dtype).itemsize for b in buffers)
         partial = pl.pallas_call(
@@ -663,10 +709,10 @@
                 dma((zs,)),
                 dma((zs + 1,)),
                 dma((zs + 1,)),
-                dma((zs,)),
-                dma((zs,)),
-                dma((7,)),
-                dma((7,)),
+                dma((2, zs)),
+                dma((2, zs)),
+                dma((2, 7)),
+                dma((2, 7)),
             ],
             compiler_params=pltpu.CompilerParams(
                 collective_id=0,

time: 49.8 us -> 48.9 us (0.982)
  Pallas kernels: 49 us -> 48.1 us
    pallas_call x1, Pallas kernels: 47.6 us -> 46.7 us  [per_device(): pl.pallas_call(functools.partial(kernel, devs, pool), out_shape=(jax.Shap...]
where the time goes in v3:
time: 48.9 us; the launch traced here: 48.7 us
  Pallas kernels  48.1 us (98%)
  between operations  0.64 us (1%)
    pallas_call x1, Pallas kernels, per_device(): pl.pallas_call(functools.partial(kernel, devs, pool), out_shape=(jax.Shap...  46.7 us
    pallas_call x1, Pallas kernels, per_device(): pl.pallas_call(place_outputs, out_shape=(jax.ShapeDtypeStruct((owned, ROW...  1.4 us

profile of v3, /device:TPU:0, one launch (start us, length us, event | category | flops | bytes accessed | tf_op | source)
XLA Modules:
  0.0 48.7 jit_solution(14663880068511530602)
XLA Ops:
  0.6 46.7 %shard_map.85 = (f32[2,1024,128]{2,1,0:T(8,128)S(1)}, f32[4,512,128]{2,1,0:T(8,128)S(1)}, f32[1,512]{1,0:T(1,128)S(1)}) custom-call(s32[32]{0:T(128)} %owner_hbm.1, bf16[128,32,128]{2,1,0:T(8,128)(2,1)} %x_hbm.1, s32[4,32,128]{2,1,0:T(8,128)} %bitcast.3, s32[32,128]{1,0:T(8,128)} %bitcast.4, bf16[128,512]{1,0:T(8,128)(2,1)} %acts_hbm.1, bf16[128,512]{1,0:T(8,128)(2,1)} %cot_hbm.1), custom_call_target="tpu_custom_call" | custom-call | tf_op jit(solution)/shard_map/pallas_call | solution.py:684
  47.3 1.4 %shard_map.86 = (f32[2,1024,128]{2,1,0:T(8,128)}, f32[512,512]{1,0:T(8,128)}, f32[1,512]{1,0:T(1,128)}) custom-call(f32[2,1024,128]{2,1,0:T(8,128)S(1)} %get-tuple-element.9.table_in, f32[4,512,128]{2,1,0:T(8,128)S(1)} %get-tuple-element.10.whole_in, f32[1,512]{1,0:T(1,128)S(1)} %get-tuple-element.11.bias_in), custom_call_target="tpu_custom_call" | custom-call | tf_op jit(solution)/shard_map/pallas_call | solution.py:731

commit v4 on v3

--- a/solution.py
+++ b/solution.py
@@ -11,7 +11,7 @@
 ROWS = 1024
 SPAN = 128
 MESH = pl.DeviceIdType.MESH
-CHUNKS = 4
+CHUNKS = 1
 PAD = 8
 GROUP = 16
 LEVELS = 32767.0
@@ -404,10 +404,8 @@
                 copy.wait_recv()
 
         total = lax.fori_loop(1, zs, lambda i, run: run + zbuf[i], zbuf[0])
-        total = total.reshape(piece // 8, 8, 128)
-        top = jnp.maximum(jnp.max(jnp.abs(total), axis=0), TINY)
-        code = jnp.round(total * (LEVELS / top)).astype(jnp.int32)
-        coded[place, grp, z] = code.reshape(piece, 128).astype(jnp.int16)
+        top = jnp.maximum(jnp.max(jnp.abs(total), axis=0, keepdims=True), TINY)
+        coded[place, grp, z] = jnp.round(total * (LEVELS / top)).astype(jnp.int32).astype(jnp.int16)
         steps[place, grp, z] = top * (1.0 / LEVELS)
         bp[2] = lax.fori_loop(1, zs, lambda i, run: run + bz[i], bz[0])
 
@@ -473,9 +471,8 @@
         @pl.loop(0, zs)
         def _(i):
             code = coded[tile, which, i].astype(jnp.int32).astype(jnp.float32)
-            value = code.reshape(piece // 8, 8, 128) * steps[tile, which, i]
             rows = pl.ds(pl.multiple_of(which * half + i * piece, 8), piece)
-            whole[tile, rows, :] = value.reshape(piece, 128)
+            whole[tile, rows, :] = code * steps[tile, which, i]
 
     def accumulate(side, first, second):
         marks = jnp.concatenate(
@@ -515,16 +512,16 @@
     build(recv.at[0, me], me)
     forward(me).start()
     level_start(1)
+    column_start(2)
     level_start(2)
     level_start(3)
     column_start(1)
-    column_start(2)
     column_start(3)
     column_pass(1, close)
+    plane_finish()
     column_pass(1, rest)
     level_pass(1)
     table_ref[...] = jnp.zeros(table_ref.shape, jnp.float32)
-    plane_finish()
     line_pass(0, close)
     y_finish()
     z_start()
@@ -538,14 +535,14 @@
     zg_start()
     column_pass(2, rest)
     line_pass(1, rest)
+    zg_finish()
+    gather_start(0, 1, 3)
     column_pass(3, close)
     column_pass(3, rest)
     close(functools.partial(pair, 0, 0))
     rest(functools.partial(pair, 0, 0))
     far_pair(0, z)
     line_pass(2, close)
-    zg_finish()
-    gather_start(0, 1, 3)
     line_pass(2, rest)
     pair(0, 1, z)
     close(functools.partial(far_pair, 0))
@@ -678,7 +675,7 @@
             pltpu.VMEM((zs, 8, 128), f32),
             pltpu.VMEM((8, 128), f32),
             pltpu.VMEM((4, 2, zs, half // zs, 128), jnp.int16),
-            pltpu.VMEM((4, 2, zs, 8, 128), f32),
+            pltpu.VMEM((4, 2, zs, 1, 128), f32),
         ]
         held = sum(math.prod(b.shape) * jnp.dtype(b.dtype).itemsize for b in buffers)
         partial = pl.pallas_call(

time: 48.9 us -> 47.1 us (0.963)
  Pallas kernels: 48.1 us -> 46.3 us
    pallas_call x1, Pallas kernels: 46.7 us -> 44.9 us  [per_device(): pl.pallas_call(functools.partial(kernel, devs, pool), out_shape=(jax.Shap...]
where the time goes in v4:
time: 47.1 us; the launch traced here: 46.9 us
  Pallas kernels  46.3 us (98%)
  between operations  0.64 us (1%)
    pallas_call x1, Pallas kernels, per_device(): pl.pallas_call(functools.partial(kernel, devs, pool), out_shape=(jax.Shap...  44.9 us
    pallas_call x1, Pallas kernels, per_device(): pl.pallas_call(place_outputs, out_shape=(jax.ShapeDtypeStruct((owned, ROW...  1.4 us

profile of v4, /device:TPU:0, one launch (start us, length us, event | category | flops | bytes accessed | tf_op | source)
XLA Modules:
  0.0 46.9 jit_solution(671865506454148188)
XLA Ops:
  0.6 44.9 %shard_map.85 = (f32[2,1024,128]{2,1,0:T(8,128)S(1)}, f32[4,512,128]{2,1,0:T(8,128)S(1)}, f32[1,512]{1,0:T(1,128)S(1)}) custom-call(s32[32]{0:T(128)} %owner_hbm.1, bf16[128,32,128]{2,1,0:T(8,128)(2,1)} %x_hbm.1, s32[4,32,128]{2,1,0:T(8,128)} %bitcast.3, s32[32,128]{1,0:T(8,128)} %bitcast.4, bf16[128,512]{1,0:T(8,128)(2,1)} %acts_hbm.1, bf16[128,512]{1,0:T(8,128)(2,1)} %cot_hbm.1), custom_call_target="tpu_custom_call" | custom-call | tf_op jit(solution)/shard_map/pallas_call | solution.py:681
  45.5 1.4 %shard_map.86 = (f32[2,1024,128]{2,1,0:T(8,128)}, f32[512,512]{1,0:T(8,128)}, f32[1,512]{1,0:T(1,128)}) custom-call(f32[2,1024,128]{2,1,0:T(8,128)S(1)} %get-tuple-element.9.table_in, f32[4,512,128]{2,1,0:T(8,128)S(1)} %get-tuple-element.10.whole_in, f32[1,512]{1,0:T(1,128)S(1)} %get-tuple-element.11.bias_in), custom_call_target="tpu_custom_call" | custom-call | tf_op jit(solution)/shard_map/pallas_call | solution.py:728

commit v5 on v4

--- a/solution.py
+++ b/solution.py
@@ -546,18 +546,18 @@
     line_pass(2, rest)
     pair(0, 1, z)
     close(functools.partial(far_pair, 0))
-    rest(functools.partial(far_pair, 0))
     gather_wait(0)
     gather_start(2, 4)
     decode(place, grp)
     decode(place, other)
+    rest(functools.partial(far_pair, 0))
     line_pass(3, close)
     line_pass(3, rest)
-    close(functools.partial(pair, 0, 1))
-    rest(functools.partial(pair, 0, 1))
     gather_wait(1)
     gather_start(5)
     decode(places[2], grp)
+    close(functools.partial(pair, 0, 1))
+    rest(functools.partial(pair, 0, 1))
     far_pair(1, z)
     gather_wait(2)
     gather_start(6)

time: 47.1 us -> 47.1 us (level)
  no operation moved by 1% of the time
where the time goes in v5:
time: 47.1 us; the launch traced here: 46.9 us
  Pallas kernels  46.3 us (98%)
  between operations  0.64 us (1%)
    pallas_call x1, Pallas kernels, per_device(): pl.pallas_call(functools.partial(kernel, devs, pool), out_shape=(jax.Shap...  44.9 us
    pallas_call x1, Pallas kernels, per_device(): pl.pallas_call(place_outputs, out_shape=(jax.ShapeDtypeStruct((owned, ROW...  1.4 us

profile of v5, /device:TPU:0, one launch (start us, length us, event | category | flops | bytes accessed | tf_op | source)
XLA Modules:
  0.0 46.9 jit_solution(15956367135144189883)
XLA Ops:
  0.6 44.9 %shard_map.85 = (f32[2,1024,128]{2,1,0:T(8,128)S(1)}, f32[4,512,128]{2,1,0:T(8,128)S(1)}, f32[1,512]{1,0:T(1,128)S(1)}) custom-call(s32[32]{0:T(128)} %owner_hbm.1, bf16[128,32,128]{2,1,0:T(8,128)(2,1)} %x_hbm.1, s32[4,32,128]{2,1,0:T(8,128)} %bitcast.3, s32[32,128]{1,0:T(8,128)} %bitcast.4, bf16[128,512]{1,0:T(8,128)(2,1)} %acts_hbm.1, bf16[128,512]{1,0:T(8,128)(2,1)} %cot_hbm.1), custom_call_target="tpu_custom_call" | custom-call | tf_op jit(solution)/shard_map/pallas_call | solution.py:681
  45.5 1.4 %shard_map.86 = (f32[2,1024,128]{2,1,0:T(8,128)}, f32[512,512]{1,0:T(8,128)}, f32[1,512]{1,0:T(1,128)}) custom-call(f32[2,1024,128]{2,1,0:T(8,128)S(1)} %get-tuple-element.9.table_in, f32[4,512,128]{2,1,0:T(8,128)S(1)} %get-tuple-element.10.whole_in, f32[1,512]{1,0:T(1,128)S(1)} %get-tuple-element.11.bias_in), custom_call_target="tpu_custom_call" | custom-call | tf_op jit(solution)/shard_map/pallas_call | solution.py:728
